TPU v7x, 32 devices: a whole 2x2x4 slice. The times are simulated.
32 devices in a mesh: groups: 2 (over x), seq: 16 (over z, y, core).
Axes of the slice: x: 2, y: 2, z: 4, core: 2. Of those that a mesh axis runs over, the one named last changes fastest.
Arguments:
- activations: bfloat16 [512, 14336], P(('groups', 'seq')), parts along dimension 0, may hold values from -6 to 6
- out_grads: bfloat16 [512, 2048], P(('groups', 'seq')), parts along dimension 0, may hold values from -6 to 6
- query_ids: int32 [512], P(('groups', 'seq')), parts along dimension 0, may hold values from 0 to 2, never falling along the last dimension, each value on 1 to 128 neighbouring positions
- act_basis: bfloat16 [64, 224, 224], P('seq'), may hold values from -0.375 to 0.375
- grad_basis: bfloat16 [2048, 2048], P(None, 'seq'), may hold values from -0.125 to 0.125
- eigenvalues: float32 [2048, 14336], P(None, 'seq'), may hold values from 8 to 80
Outputs:
- precond: bfloat16 [6, 2048, 14336], P('groups', None, 'seq'), parts along dimension 0
There are 2 independent parts, one for each index of `groups`. A program takes and returns all parts, laid end to end along the dimension named above; an argument that names none is the same for every part. Nothing has to cross between parts.
Inputs may be any that keep to these rules, and one draw needn't show every extreme that they name: `query_ids`: query ids never fall along the tokens; each of the 3 queries has at least one and at most 128 tokens.
All inputs are finite; a program needn't handle non-finite values.
Results may differ from a plain program's by a relative error of at most 0.006.
Values may be sent and summed in bfloat16 or wider, within the bound.
A program may use at most 128 MiB of HBM per device.

v0:
```python
import jax
import jax.numpy as jnp
from jax import lax
from jax.sharding import PartitionSpec as P

QUERIES = 3


def shards(activations, out_grads, query_ids, act_basis, grad_basis, eigenvalues):
    local_blocks = act_basis.shape[0]
    block_order = act_basis.shape[1]
    out_units = grad_basis.shape[0]
    columns = lax.all_to_all(activations, "seq", split_axis=1, concat_axis=0, tiled=True)
    all_tokens = columns.shape[0]
    local_width = local_blocks * block_order
    rotated_act = jnp.einsum(
        "tbi,bik->tbk",
        columns.reshape(all_tokens, local_blocks, block_order),
        act_basis,
        preferred_element_type=jnp.float32,
    )
    rotated_act = rotated_act.astype(jnp.bfloat16).reshape(all_tokens, local_width)
    full_basis = lax.all_gather(grad_basis, "seq", axis=1, tiled=True)
    own_rotated = jnp.dot(out_grads, full_basis, preferred_element_type=jnp.float32).astype(
        jnp.bfloat16
    )
    rotated_grad, token_query = (
        lax.all_gather(own_rotated, "seq", axis=0, tiled=True),
        lax.all_gather(query_ids, "seq", axis=0, tiled=True),
    )
    selector = (token_query[:, None] == jnp.arange(QUERIES, dtype=jnp.int32)[None, :]).astype(
        jnp.bfloat16
    )
    selected = (rotated_act[:, None, :] * selector[:, :, None]).reshape(
        all_tokens, QUERIES * local_width
    )
    moments = lax.dot_general(
        rotated_grad, selected, (((0,), (0,)), ((), ())), preferred_element_type=jnp.float32
    )
    scaled = (moments.reshape(out_units, QUERIES, local_width) / eigenvalues[:, None, :]).astype(
        jnp.bfloat16
    )
    rotated_back = jnp.einsum(
        "dqbk,bik->dqbi",
        scaled.reshape(out_units, QUERIES, local_blocks, block_order),
        act_basis,
        preferred_element_type=jnp.float32,
    )
    rotated_back = rotated_back.astype(jnp.bfloat16).reshape(out_units, QUERIES * local_width)
    result = jnp.dot(full_basis, rotated_back, preferred_element_type=jnp.float32)
    result = result.reshape(out_units, QUERIES, local_width)
    return jnp.transpose(result, (1, 0, 2)).astype(jnp.bfloat16)


def solution(mesh):
    return jax.shard_map(
        shards,
        mesh=mesh,
        in_specs=(
            P(("groups", "seq"), None),
            P(("groups", "seq"), None),
            P(("groups", "seq")),
            P("seq", None, None),
            P(None, "seq"),
            P(None, "seq"),
        ),
        out_specs=P("groups", None, "seq"),
        check_vma=False,
    )
```

profile of v0, /device:TPU:0, one launch (start us, length us, event | category | flops | bytes accessed | tf_op | source)
XLA Modules:
  0.0 207.3 jit_solution(7658103903438815733)
XLA Ops:
  6.5 0.0 copy-start
  6.5 0.0 copy-start.2
  6.5 0.0 all-gather.3.cloned.1.call-start
  6.5 0.7 all-gather.3.cloned.1.call-update
  7.3 0.0 all-gather.5.cloned.1.call-start
  7.3 82.6 %all-gather.3.cloned.1.call-done = bf16[2048,2048]{1,0:T(8,128)(2,1)} async-done(((bf16[2048,128]{1,0:T(8,128)(2,1)}), bf16[2048,2048]{1,0:T(8,128)(2,1)}) %all-gather.3.cloned.1.call-update) | async-done | bytes 8388624 | tf_op jit(solution)/shard_map/all_gather | solution.py:23
  90.0 5.2 %convolution_convert_fusion.1 = bf16[16,2048]{1,0:T(8,128)(2,1)} fusion(bf16[16,2048]{1,0:T(8,128)(2,1)} %param.7, bf16[2048,2048]{1,0:T(8,128)(2,1)} %all-gather.3.cloned.1.call-done), kind=kOutput, calls=%fused_computation.5 | convolution fusion | flops 134250496 | bytes 8519680 | tf_op jit(solution)/shard_map/dot_general | solution.py:24
  95.2 0.0 copy-start.4
  95.2 0.0 copy-start.3
  95.2 0.0 all-gather.5.cloned.1.call-update
  95.2 0.0 copy-done.2
  95.2 0.8 copy.29
  96.0 3.6 %all-to-all-start = ((bf16[16,16,896]{2,0,1:T(8,128)(2,1)}), bf16[16,16,896]{2,0,1:T(8,128)(2,1)S(1)}, u32[]{:S(2)}, u32[]{:S(2)}) async-start(bf16[16,16,896]{2,0,1:T(8,128)(2,1)} %bitcast.36), calls=%async_computation | async-start | bytes 917504 | tf_op jit(solution)/shard_map/all_to_all | solution.py:13
  99.6 8.6 %copy.15 = f32[2048,896]{0,1:T(8,128)} copy(f32[2048,896]{1,0:T(8,128)} %param.11) | data formatting | bytes 14680064 | tf_op args[5]
  108.2 0.0 copy-done.4
  108.2 0.6 dynamic-slice
  109.4 0.0 copy-done.3
  109.4 0.2 dynamic-update-slice
  109.6 12.4 %all-reduce = s32[256]{0:T(256)S(1)} all-reduce(s32[256]{0:T(256)S(1)} %dynamic-update-slice), channel_id=1, replica_groups=mesh['groups'=2,'seq'=16] {'seq'}, use_global_device_ids=true, to_apply=%add | all-reduce | flops 256 | bytes 2048
  122.1 0.0 all-to-all-done
  122.1 0.5 reshape.45
  122.6 0.0 copy-done
  122.6 0.3 convolution_convert_fusion.2
  122.9 10.5 %all-gather.5.cloned.1.call-done = bf16[256,2048]{1,0:T(8,128)(2,1)} async-done(((bf16[16,2048]{1,0:T(8,128)(2,1)}), bf16[256,2048]{1,0:T(8,128)(2,1)}) %all-gather.5.cloned.1.call-update) | async-done | bytes 1048592 | tf_op jit(solution)/shard_map/all_gather | solution.py:28
  133.5 8.2 %divide_convert_fusion = bf16[2048,3,896]{0,2,1:T(8,128)(2,1)} fusion(f32[2048,896]{0,1:T(8,128)} %copy.15, bf16[256,2048]{1,0:T(8,128)(2,1)} %all-gather.5.cloned.1.call-done, bf16[256,3]{0,1:T(4,128)(2,1)S(1)} %fusion.11, bf16[256,896]{0,1:T(8,128)(2,1)S(1)} %bitcast.42), kind=kOutput, calls=%fused_computation | convolution fusion | flops 2832334848 | bytes 19858944 | tf_op jit(solution)/shard_map/dot_general | solution.py:37
  141.6 11.3 %convert_bitcast_fusion = bf16[2048,3,4,224]{0,3,1,2:T(8,128)(2,1)} fusion(bf16[2048,3,4,224]{0,3,2,1:T(8,128)(2,1)} %bitcast.37, bf16[4,224,224]{2,1,0:T(8,128)(2,1)S(1)} %copy-done), kind=kOutput, calls=%fused_computation.4 | convolution fusion | flops 2471755776 | bytes 22421504 | tf_op jit(solution)/shard_map/dqbk,bik->dqbi/dot_general | solution.py:43
  153.0 5.8 %copy.17 = bf16[2048,3,4,224]{0,3,2,1:T(8,128)(2,1)S(1)} copy(bf16[2048,3,4,224]{0,3,1,2:T(8,128)(2,1)} %convert_bitcast_fusion) | data formatting | bytes 22020096 | tf_op jit(solution)/shard_map/convert_element_type | solution.py:49
  158.8 27.0 %convolution_convert_fusion = bf16[2688,2048]{1,0:T(8,128)(2,1)} fusion(bf16[2048,2688]{0,1:T(8,128)(2,1)S(1)} %bitcast.38, bf16[2048,2048]{1,0:T(8,128)(2,1)} %all-gather.3.cloned.1.call-done), kind=kOutput, calls=%fused_computation.1 | convolution fusion | flops 22554083328 | bytes 30408704 | tf_op jit(solution)/shard_map/dot_general | solution.py:50
  185.8 0.0 copy-start.1
  185.8 14.7 %copy.18 = bf16[2048,3,896]{2,0,1:T(8,128)(2,1)} copy(bf16[2048,3,896]{0,2,1:T(8,128)(2,1)} %bitcast.39) | data formatting | bytes 22020096 | tf_op jit(solution)/shard_map/convert_element_type | solution.py:52
  200.5 0.0 copy-done.1
  (2 shorter events, 0.0 us)
Async XLA Ops:
  6.5 116.0 %copy-start = (bf16[4,224,224]{2,1,0:T(8,128)(2,1)S(1)}, bf16[4,224,224]{2,1,0:T(8,128)(2,1)}, u32[]{:S(2)}) copy-start(bf16[4,224,224]{2,1,0:T(8,128)(2,1)} %param.9) | copy-start | bytes 1204228
  6.5 88.7 %copy-start.2 = (bf16[16,14336]{1,0:T(8,128)(2,1)S(1)}, bf16[16,14336]{1,0:T(8,128)(2,1)}, u32[]{:S(2)}) copy-start(bf16[16,14336]{1,0:T(8,128)(2,1)} %param.6) | copy-start | bytes 1376260
  6.5 83.4 %all-gather.3.cloned.1.call-start = ((), (), s32[]{:S(2)}) async-start(), calls=%async_computation.1 | async-start | bytes 8912896 | tf_op jit(solution)/shard_map/all_gather | solution.py:23
  7.3 126.2 %all-gather.5.cloned.1.call-start = ((), (), s32[]{:S(2)}) async-start(), calls=%async_computation.2 | async-start | bytes 1114112 | tf_op jit(solution)/shard_map/all_gather | solution.py:28
  95.2 13.0 %copy-start.4 = (u32[32]{0:T(128)S(1)}, u32[32]{0:T(128)}, u32[]{:S(2)}) copy-start(u32[32]{0:T(128)} %constant.6) | copy-start | bytes 388
  95.2 14.2 %copy-start.3 = (s32[16]{0:T(128)S(1)}, s32[16]{0:T(128)}, u32[]{:S(2)}) copy-start(s32[16]{0:T(128)} %param.8) | copy-start | bytes 196
  96.0 26.0 %all-to-all-start = ((bf16[16,16,896]{2,0,1:T(8,128)(2,1)}), bf16[16,16,896]{2,0,1:T(8,128)(2,1)S(1)}, u32[]{:S(2)}, u32[]{:S(2)}) async-start(bf16[16,16,896]{2,0,1:T(8,128)(2,1)} %bitcast.36), calls=%async_computation | async-start | bytes 917504 | tf_op jit(solution)/shard_map/all_to_all | solution.py:13
  185.8 14.7 %copy-start.1 = (bf16[4,224,224]{2,1,0:T(8,128)(2,1)S(1)}, bf16[4,224,224]{2,1,0:T(8,128)(2,1)}, u32[]{:S(2)}) copy-start(bf16[4,224,224]{2,1,0:T(8,128)(2,1)} %param.9) | copy-start | bytes 1204228
Sparse Core Ops, SparseCore 0:
  9.5 80.4 all-gather.2
  95.3 38.0 all-gather.4
where the time goes:
time: 208 us; the launch traced here: 207 us
  waiting for transfers between devices  93.9 us (45%)
  matrix products  52.1 us (25%)
  local copies, waits for them, and re-layouts  31.2 us (15%)
  between operations  14 us (7%)
  blocking collectives  12.4 us (6%)
  starting transfers between devices  3.6 us (2%)
    all_gather x1, waiting for transfers between devices, shards(): full_basis = lax.all_gather(grad_basis, 'seq', axis=1, tiled=True)  82.6 us
    dot_general x1, matrix products, shards(): jnp.dot(full_basis, rotated_back, preferred_element_type=jnp.float32)  27 us
    convert_element_type x1, local copies, waits for them, and re-layouts, shards(): return jnp.transpose(result, (1, 0, 2)).astype(jnp.bfloat16)  14.7 us
    unnamed x1, blocking collectives  12.4 us
    dot_general x1, matrix products, shards(): jnp.einsum('dqbk,bik->dqbi', scaled.reshape(out_units, QUERIES, local_blo...  11.3 us
    all_gather x1, waiting for transfers between devices, shards(): lax.all_gather(own_rotated, 'seq', axis=0, tiled=True)  10.5 us
    unnamed x14, local copies, waits for them, and re-layouts  9.46 us
    dot_general x1, matrix products, shards(): lax.dot_general(rotated_grad, selected, (((0,), (0,)), ((), ())), preferr...  8.18 us
  transfers between devices with their start and end apart: 3, of which 2 were waited for; matrix products, arithmetic and copies ran while one was open for 5% of the time, Pallas kernels for 0%

commit v1 on v0

--- a/solution.py
+++ b/solution.py
@@ -20,7 +20,9 @@
         preferred_element_type=jnp.float32,
     )
     rotated_act = rotated_act.astype(jnp.bfloat16).reshape(all_tokens, local_width)
-    full_basis = lax.all_gather(grad_basis, "seq", axis=1, tiled=True)
+    full_basis = jnp.concatenate(
+        lax.all_to_all(jnp.stack([grad_basis] * lax.axis_size("seq")), "seq", 0, 0), axis=1
+    )
     own_rotated = jnp.dot(out_grads, full_basis, preferred_element_type=jnp.float32).astype(
         jnp.bfloat16
     )

time: 208 us -> 321 us (1.54)
  blocking collectives: 12.4 us -> 202 us
  waiting for transfers between devices: 93.9 us -> 10.8 us
  local copies, waits for them, and re-layouts: 31.2 us -> 37 us
    all_to_all x0 -> x1, blocking collectives: none -> 189 us  [shards(): lax.all_to_all(jnp.stack([grad_basis] * lax.axis_size('seq')), 'seq', 0, 0)]
    all_gather x1 -> x0, waiting for transfers between devices: 82.6 us -> none  [shards(): full_basis = lax.all_gather(grad_basis, 'seq', axis=1, tiled=True)]
    unnamed x14 -> x19, local copies, waits for them, and re-layouts: 9.46 us -> 14.2 us
  transfers between devices with their start and end apart: 3 -> 2, of which waited for: 2 -> 1; matrix products, arithmetic and copies ran while one was open for 5% -> 3% of each run, Pallas kernels for 0% -> 0%
where the time goes in v1:
time: 321 us; the launch traced here: 320 us
  blocking collectives  202 us (63%)
  matrix products  51 us (16%)
  local copies, waits for them, and re-layouts  37 us (12%)
  between operations  14.1 us (4%)
  waiting for transfers between devices  10.8 us (3%)
  starting transfers between devices  5.72 us (2%)
    all_to_all x1, blocking collectives, shards(): lax.all_to_all(jnp.stack([grad_basis] * lax.axis_size('seq')), 'seq', 0, 0)  189 us
    dot_general x1, matrix products, shards(): jnp.dot(full_basis, rotated_back, preferred_element_type=jnp.float32)  28.2 us
    convert_element_type x1, local copies, waits for them, and re-layouts, shards(): return jnp.transpose(result, (1, 0, 2)).astype(jnp.bfloat16)  14.7 us
    unnamed x19, local copies, waits for them, and re-layouts  14.2 us
    unnamed x1, blocking collectives  12.5 us
    dot_general x1, matrix products, shards(): jnp.einsum('dqbk,bik->dqbi', scaled.reshape(out_units, QUERIES, local_blo...  11.4 us
    all_gather x1, waiting for transfers between devices, shards(): lax.all_gather(own_rotated, 'seq', axis=0, tiled=True)  10.8 us
    dot_general x1, matrix products, shards(): lax.dot_general(rotated_grad, selected, (((0,), (0,)), ((), ())), preferr...  8.18 us
  transfers between devices with their start and end apart: 2, of which 1 were waited for; matrix products, arithmetic and copies ran while one was open for 3% of the time, Pallas kernels for 0%

profile of v1, /device:TPU:0, one launch (start us, length us, event | category | flops | bytes accessed | tf_op | source)
XLA Modules:
  0.0 320.5 jit_solution(4088509647162580671)
XLA Ops:
  6.5 0.0 copy-start
  6.5 0.0 all-gather.2.cloned.1.call-start
  6.5 1.3 copy.12
  7.8 0.0 copy-start.4
  7.9 1.1 stack.2
  8.9 0.0 copy-start.3
  8.9 189.3 %all_to_all.21 = bf16[16,2048,128]{1,2,0:T(8,128)(2,1)S(1)} all-to-all(bf16[16,2048,128]{1,2,0:T(8,128)(2,1)S(1)} %stack.2), channel_id=1, replica_groups=mesh['groups'=2,'seq'=16] {'seq'}, dimensions={0} | all-to-all | bytes 16777216 | tf_op jit(solution)/shard_map/all_to_all | solution.py:24
  198.3 0.0 copy-start.2
  198.3 3.3 %copy-done.2 = bf16[16,2048,128]{1,2,0:T(8,128)(2,1)} copy-done((bf16[16,2048,128]{1,2,0:T(8,128)(2,1)}, bf16[16,2048,128]{1,2,0:T(8,128)(2,1)S(1)}, u32[]{:S(2)}) %copy-start.2) | copy-done | bytes 8388632
  201.6 0.0 copy-done.4
  201.6 0.0 copy-start.6
  201.6 0.0 copy-start.5
  201.6 2.9 convolution_convert_fusion.1
  204.5 0.0 all-gather.2.cloned.1.call-update
  204.5 0.0 copy-done.3
  204.5 0.8 copy.30
  205.3 5.7 %all-to-all-start.1 = ((bf16[16,16,896]{2,0,1:T(8,128)(2,1)}), bf16[16,16,896]{2,0,1:T(8,128)(2,1)S(1)}, u32[]{:S(2)}, u32[]{:S(2)}) async-start(bf16[16,16,896]{2,0,1:T(8,128)(2,1)} %bitcast.39), calls=%async_computation.1 | async-start | bytes 917504 | tf_op jit(solution)/shard_map/all_to_all | solution.py:13
  211.0 8.7 %copy.16 = f32[2048,896]{0,1:T(8,128)} copy(f32[2048,896]{1,0:T(8,128)} %param.11) | data formatting | bytes 14680064 | tf_op args[5]
  219.7 0.0 copy-done.6
  219.7 0.6 dynamic-slice
  221.0 0.0 copy-done.5
  221.0 0.2 dynamic-update-slice
  221.3 12.5 %all-reduce = s32[256]{0:T(256)S(1)} all-reduce(s32[256]{0:T(256)S(1)} %dynamic-update-slice), channel_id=1, replica_groups=mesh['groups'=2,'seq'=16] {'seq'}, use_global_device_ids=true, to_apply=%add | all-reduce | flops 256 | bytes 2048
  233.7 0.0 all-to-all-done.1
  233.7 0.5 reshape.55
  234.2 0.0 copy-done
  234.2 0.3 convolution_convert_fusion.2
  234.6 10.8 %all-gather.2.cloned.1.call-done = bf16[256,2048]{1,0:T(8,128)(2,1)} async-done(((bf16[16,2048]{1,0:T(8,128)(2,1)}), bf16[256,2048]{1,0:T(8,128)(2,1)}) %all-gather.2.cloned.1.call-update) | async-done | bytes 1048592 | tf_op jit(solution)/shard_map/all_gather | solution.py:30
  245.4 8.2 %divide_convert_fusion = bf16[2048,3,896]{0,2,1:T(8,128)(2,1)} fusion(f32[2048,896]{0,1:T(8,128)} %copy.16, bf16[256,2048]{1,0:T(8,128)(2,1)} %all-gather.2.cloned.1.call-done, bf16[256,3]{0,1:T(4,128)(2,1)S(1)} %fusion.11, bf16[256,896]{0,1:T(8,128)(2,1)S(1)} %bitcast.47), kind=kOutput, calls=%fused_computation | convolution fusion | flops 2832334848 | bytes 19858944 | tf_op jit(solution)/shard_map/dot_general | solution.py:39
  253.6 11.4 %convert_bitcast_fusion = bf16[2048,3,4,224]{0,3,1,2:T(8,128)(2,1)} fusion(bf16[2048,3,4,224]{0,3,2,1:T(8,128)(2,1)} %bitcast.42, bf16[4,224,224]{2,1,0:T(8,128)(2,1)S(1)} %copy-done), kind=kOutput, calls=%fused_computation.4 | convolution fusion | flops 2471755776 | bytes 22421504 | tf_op jit(solution)/shard_map/dqbk,bik->dqbi/dot_general | solution.py:45
  264.9 5.8 %copy.18 = bf16[2048,3,4,224]{0,3,2,1:T(8,128)(2,1)S(1)} copy(bf16[2048,3,4,224]{0,3,1,2:T(8,128)(2,1)} %convert_bitcast_fusion) | data formatting | bytes 22020096 | tf_op jit(solution)/shard_map/convert_element_type | solution.py:51
  270.7 28.2 %convolution_convert_fusion = bf16[2688,2048]{1,0:T(8,128)(2,1)} fusion(bf16[2048,2688]{0,1:T(8,128)(2,1)S(1)} %bitcast.43, bf16[2048,2048]{0,1:T(8,128)(2,1)} %bitcast.41), kind=kOutput, calls=%fused_computation.1 | convolution fusion | flops 22554083328 | bytes 30408704 | tf_op jit(solution)/shard_map/dot_general | solution.py:52
  298.9 0.0 copy-start.1
  298.9 14.7 %copy.19 = bf16[2048,3,896]{2,0,1:T(8,128)(2,1)} copy(bf16[2048,3,896]{0,2,1:T(8,128)(2,1)} %bitcast.44) | data formatting | bytes 22020096 | tf_op jit(solution)/shard_map/convert_element_type | solution.py:54
  313.6 0.0 copy-done.1
  (2 shorter events, 0.0 us)
Async XLA Ops:
  6.5 227.7 %copy-start = (bf16[4,224,224]{2,1,0:T(8,128)(2,1)S(1)}, bf16[4,224,224]{2,1,0:T(8,128)(2,1)}, u32[]{:S(2)}) copy-start(bf16[4,224,224]{2,1,0:T(8,128)(2,1)} %param.9) | copy-start | bytes 1204228
  6.5 238.8 %all-gather.2.cloned.1.call-start = ((), (), s32[]{:S(2)}) async-start(), calls=%async_computation.2 | async-start | bytes 1114112 | tf_op jit(solution)/shard_map/all_gather | solution.py:30
  7.8 193.7 %copy-start.4 = (bf16[16,2048]{1,0:T(8,128)(2,1)S(1)}, bf16[16,2048]{1,0:T(8,128)(2,1)}, u32[]{:S(2)}) copy-start(bf16[16,2048]{1,0:T(8,128)(2,1)} %param.7) | copy-start | bytes 196612
  8.9 195.6 %copy-start.3 = (bf16[16,14336]{1,0:T(8,128)(2,1)S(1)}, bf16[16,14336]{1,0:T(8,128)(2,1)}, u32[]{:S(2)}) copy-start(bf16[16,14336]{1,0:T(8,128)(2,1)} %param.6) | copy-start | bytes 1376260
  198.3 3.3 %copy-start.2 = (bf16[16,2048,128]{1,2,0:T(8,128)(2,1)}, bf16[16,2048,128]{1,2,0:T(8,128)(2,1)S(1)}, u32[]{:S(2)}) copy-start(bf16[16,2048,128]{1,2,0:T(8,128)(2,1)S(1)} %all_to_all.21) | copy-start | bytes 25165828
  201.6 18.1 %copy-start.6 = (u32[32]{0:T(128)S(1)}, u32[32]{0:T(128)}, u32[]{:S(2)}) copy-start(u32[32]{0:T(128)} %constant.6) | copy-start | bytes 388
  201.6 19.4 %copy-start.5 = (s32[16]{0:T(128)S(1)}, s32[16]{0:T(128)}, u32[]{:S(2)}) copy-start(s32[16]{0:T(128)} %param.8) | copy-start | bytes 196
  205.3 28.4 %all-to-all-start.1 = ((bf16[16,16,896]{2,0,1:T(8,128)(2,1)}), bf16[16,16,896]{2,0,1:T(8,128)(2,1)S(1)}, u32[]{:S(2)}, u32[]{:S(2)}) async-start(bf16[16,16,896]{2,0,1:T(8,128)(2,1)} %bitcast.39), calls=%async_computation.1 | async-start | bytes 917504 | tf_op jit(solution)/shard_map/all_to_all | solution.py:13
  298.9 14.7 %copy-start.1 = (bf16[4,224,224]{2,1,0:T(8,128)(2,1)S(1)}, bf16[4,224,224]{2,1,0:T(8,128)(2,1)}, u32[]{:S(2)}) copy-start(bf16[4,224,224]{2,1,0:T(8,128)(2,1)} %param.9) | copy-start | bytes 1204228
Sparse Core Ops, SparseCore 0:
  204.6 40.7 all-gather.1
